TPU v7x, 32 devices: a whole 2x2x4 slice. The times are simulated.
32 devices in a mesh: freq: 2 (over x), base: 4 (over y, core), pix: 4 (over z).
Axes of the slice: x: 2, y: 2, z: 4, core: 2. Of those that a mesh axis runs over, the one named last changes fastest.
Arguments:
- sensing_operator_parts: bfloat16 [2, 4096, 2048], P('freq', 'base', 'pix'), may hold values from -1 to 1
- sampled_correlations: float32 [64, 4096], P('freq', 'base'), may hold values from -40 to 40
- first_sky_estimate: float32 [64, 4, 4, 128], P('freq', 'pix', 'base'), may hold values from -2.5 to 2.5
- patch_order_record: int32 [6, 16], P(None, 'pix'), may hold values from 0 to 15, as said below
Outputs:
- image: float32 [64, 4, 4, 128], P('freq', 'pix', 'base')
Inputs may be any that keep to these rules, and one draw needn't show every extreme that they name: `patch_order_record`: each row holds every tile number once; the tiles of rank under 4 are the same in every row.
All inputs are finite; a program needn't handle non-finite values.
Results may differ from a plain program's by a relative error of at most 0.0014.
Values may be sent and summed in bfloat16 or wider, within the bound.
A program may use at most 64 MiB of HBM per device.

v0:
```python
import jax
import jax.numpy as jnp
from jax import lax
from jax.sharding import PartitionSpec as P

CH = 64
TILE = 128
ITERS = 6


descent_stride = 0.6
lam_shrink = 0.3
eps_norm = 1e-06


def project_rows(rounded_amount, columns):
    return lax.dot_general(
        rounded_amount, columns, (((1,), (1,)), ((), ())), preferred_element_type=jnp.float32
    )


def residual_of(sampled_correlations, partial_value):
    shares = lax.psum_scatter(partial_value, "pix", scatter_dimension=1, tiled=True)
    width = shares.shape[1]
    own_rows = lax.dynamic_slice_in_dim(
        sampled_correlations, lax.axis_index("pix") * width, width, 1
    )
    return lax.all_gather((own_rows - shares).astype(jnp.bfloat16), "pix", axis=1, tiled=True)


def on_device(sensing_operator_parts, sampled_correlations, first_sky_estimate, patch_order_record):
    sensing_operator = sensing_operator_parts[0]
    chans, m_dev = sampled_correlations.shape
    share_width = first_sky_estimate.shape[3]
    tiles_share = share_width // TILE
    keep_count = tiles_share * lax.axis_size("base") * lax.axis_size("pix") // 4
    base_index = lax.axis_index("base")
    own_share = first_sky_estimate[:, 0, 0, :]
    current = own_share
    for step in range(ITERS):
        rounded_amount = current.astype(jnp.bfloat16)
        partial_value = project_rows(
            lax.all_gather(rounded_amount, "base", axis=1, tiled=True), sensing_operator
        )
        resid = residual_of(sampled_correlations, partial_value)
        gradient_portion = jnp.dot(resid, sensing_operator, preferred_element_type=jnp.float32)
        grad_share = lax.psum_scatter(gradient_portion, "base", scatter_dimension=1, tiled=True)
        moved = current + descent_stride * grad_share
        tiles = moved.reshape(chans, tiles_share, TILE)
        local_sum = jnp.sum(tiles * tiles, axis=(0, 2))
        total = lax.psum(local_sum, "freq")
        ranks = lax.dynamic_slice_in_dim(
            patch_order_record[step], base_index * tiles_share, tiles_share, 0
        )
        rms_tile = jnp.sqrt(total / (CH * TILE) + eps_norm)
        keeping = (ranks < keep_count).astype(jnp.float32)
        factor = keeping * rms_tile / (rms_tile + lam_shrink)
        current = (tiles * factor[None, :, None]).reshape(chans, share_width)
    return current.reshape(chans, 1, 1, share_width)


def solution(mesh):
    in_specs = (
        P("freq", "base", "pix"),
        P("freq", "base"),
        P("freq", "pix", "base", None),
        P(None, "pix"),
    )
    out_specs = P("freq", "pix", "base", None)
    return jax.shard_map(
        on_device, mesh=mesh, in_specs=in_specs, out_specs=out_specs, check_vma=False
    )
```

profile of v0, /device:TPU:0, one launch (start us, length us, event | category | flops | bytes accessed | tf_op | source)
XLA Modules:
  0.0 418.8 jit_solution(5193370528719612826)
XLA Ops:
  7.3 6.1 %all_gather.36 = bf16[32,512]{1,0:T(8,128)(2,1)S(1)} all-gather(bf16[32,128]{1,0:T(8,128)(2,1)S(1)} %convert_element_type.42), channel_id=1, replica_groups=mesh['freq'=2,'base'=4,'pix'=4] {'base'}, dimensions={1}, use_global_device_ids=true | all-gather | bytes 40960 | tf_op jit(solution)/shard_map/all_gather | solution.py:43
  14.6 21.3 %reduce-scatter.13.cloned.1.call-done = f32[32,256]{1,0:T(8,128)} async-done(((f32[32,1024]{1,0:T(8,128)}), f32[32,256]{1,0:T(8,128)}) %reduce-scatter.13.cloned.1.call-update) | async-done | bytes 32784 | tf_op jit(solution)/shard_map/reduce_scatter | solution.py:23
  36.7 13.1 %all_gather.37 = bf16[32,1024]{1,0:T(8,128)(2,1)S(1)} all-gather(bf16[32,256]{1,0:T(8,128)(2,1)S(1)} %subtract_convert_fusion.5), channel_id=1, replica_groups=mesh['freq'=2,'base'=4,'pix'=4] {'pix'}, dimensions={1}, use_global_device_ids=true | all-gather | bytes 81920 | tf_op jit(solution)/shard_map/all_gather | solution.py:28
  52.0 16.6 %reduce-scatter.15.cloned.1.call-done = f32[32,128]{1,0:T(8,128)} async-done(((f32[32,512]{1,0:T(8,128)}), f32[32,128]{1,0:T(8,128)}) %reduce-scatter.15.cloned.1.call-update) | async-done | bytes 16400 | tf_op jit(solution)/shard_map/reduce_scatter | solution.py:47
  83.2 19.6 %reduce-scatter.17.cloned.1.call-done = f32[32,256]{1,0:T(8,128)} async-done(((f32[32,1024]{1,0:T(8,128)}), f32[32,256]{1,0:T(8,128)}) %reduce-scatter.17.cloned.1.call-update) | async-done | bytes 32784 | tf_op jit(solution)/shard_map/reduce_scatter | solution.py:23
  103.5 13.1 %all_gather.39 = bf16[32,1024]{1,0:T(8,128)(2,1)S(1)} all-gather(bf16[32,256]{1,0:T(8,128)(2,1)S(1)} %subtract_convert_fusion.4), channel_id=1, replica_groups=mesh['freq'=2,'base'=4,'pix'=4] {'pix'}, dimensions={1}, use_global_device_ids=true | all-gather | bytes 81920 | tf_op jit(solution)/shard_map/all_gather | solution.py:28
  118.2 17.3 %reduce-scatter.19.cloned.1.call-done = f32[32,128]{1,0:T(8,128)} async-done(((f32[32,512]{1,0:T(8,128)}), f32[32,128]{1,0:T(8,128)}) %reduce-scatter.19.cloned.1.call-update) | async-done | bytes 16400 | tf_op jit(solution)/shard_map/reduce_scatter | solution.py:47
  136.9 5.5 %psum.43 = f32[1]{0:T(128)} all-reduce(f32[1]{0:T(128)} %bitcast.6), channel_id=1, replica_groups=mesh['freq'=2,'base'=4,'pix'=4] {'freq'}, use_global_device_ids=true, to_apply=%region_7.0 | all-reduce | flops 1 | bytes 8 | tf_op jit(solution)/shard_map/psum | solution.py:51
  150.1 19.6 %reduce-scatter.21.cloned.1.call-done = f32[32,256]{1,0:T(8,128)} async-done(((f32[32,1024]{1,0:T(8,128)}), f32[32,256]{1,0:T(8,128)}) %reduce-scatter.21.cloned.1.call-update) | async-done | bytes 32784 | tf_op jit(solution)/shard_map/reduce_scatter | solution.py:23
  170.5 13.1 %all_gather.41 = bf16[32,1024]{1,0:T(8,128)(2,1)S(1)} all-gather(bf16[32,256]{1,0:T(8,128)(2,1)S(1)} %subtract_convert_fusion.3), channel_id=1, replica_groups=mesh['freq'=2,'base'=4,'pix'=4] {'pix'}, dimensions={1}, use_global_device_ids=true | all-gather | bytes 81920 | tf_op jit(solution)/shard_map/all_gather | solution.py:28
  185.1 17.3 %reduce-scatter.23.cloned.1.call-done = f32[32,128]{1,0:T(8,128)} async-done(((f32[32,512]{1,0:T(8,128)}), f32[32,128]{1,0:T(8,128)}) %reduce-scatter.23.cloned.1.call-update) | async-done | bytes 16400 | tf_op jit(solution)/shard_map/reduce_scatter | solution.py:47
  203.8 5.5 %psum.44 = f32[1]{0:T(128)} all-reduce(f32[1]{0:T(128)} %bitcast.9), channel_id=1, replica_groups=mesh['freq'=2,'base'=4,'pix'=4] {'freq'}, use_global_device_ids=true, to_apply=%region_11.0 | all-reduce | flops 1 | bytes 8 | tf_op jit(solution)/shard_map/psum | solution.py:51
  217.0 19.6 %reduce-scatter.25.cloned.1.call-done = f32[32,256]{1,0:T(8,128)} async-done(((f32[32,1024]{1,0:T(8,128)}), f32[32,256]{1,0:T(8,128)}) %reduce-scatter.25.cloned.1.call-update) | async-done | bytes 32784 | tf_op jit(solution)/shard_map/reduce_scatter | solution.py:23
  237.3 13.1 %all_gather.43 = bf16[32,1024]{1,0:T(8,128)(2,1)S(1)} all-gather(bf16[32,256]{1,0:T(8,128)(2,1)S(1)} %subtract_convert_fusion.2), channel_id=1, replica_groups=mesh['freq'=2,'base'=4,'pix'=4] {'pix'}, dimensions={1}, use_global_device_ids=true | all-gather | bytes 81920 | tf_op jit(solution)/shard_map/all_gather | solution.py:28
  252.0 17.3 %reduce-scatter.27.cloned.1.call-done = f32[32,128]{1,0:T(8,128)} async-done(((f32[32,512]{1,0:T(8,128)}), f32[32,128]{1,0:T(8,128)}) %reduce-scatter.27.cloned.1.call-update) | async-done | bytes 16400 | tf_op jit(solution)/shard_map/reduce_scatter | solution.py:47
  270.7 5.5 %psum.45 = f32[1]{0:T(128)} all-reduce(f32[1]{0:T(128)} %bitcast.12), channel_id=1, replica_groups=mesh['freq'=2,'base'=4,'pix'=4] {'freq'}, use_global_device_ids=true, to_apply=%region_15.0 | all-reduce | flops 1 | bytes 8 | tf_op jit(solution)/shard_map/psum | solution.py:51
  283.9 19.6 %reduce-scatter.29.cloned.1.call-done = f32[32,256]{1,0:T(8,128)} async-done(((f32[32,1024]{1,0:T(8,128)}), f32[32,256]{1,0:T(8,128)}) %reduce-scatter.29.cloned.1.call-update) | async-done | bytes 32784 | tf_op jit(solution)/shard_map/reduce_scatter | solution.py:23
  304.2 13.1 %all_gather.45 = bf16[32,1024]{1,0:T(8,128)(2,1)S(1)} all-gather(bf16[32,256]{1,0:T(8,128)(2,1)S(1)} %subtract_convert_fusion.1), channel_id=1, replica_groups=mesh['freq'=2,'base'=4,'pix'=4] {'pix'}, dimensions={1}, use_global_device_ids=true | all-gather | bytes 81920 | tf_op jit(solution)/shard_map/all_gather | solution.py:28
  318.9 17.3 %reduce-scatter.31.cloned.1.call-done = f32[32,128]{1,0:T(8,128)} async-done(((f32[32,512]{1,0:T(8,128)}), f32[32,128]{1,0:T(8,128)}) %reduce-scatter.31.cloned.1.call-update) | async-done | bytes 16400 | tf_op jit(solution)/shard_map/reduce_scatter | solution.py:47
  337.6 5.5 %psum.46 = f32[1]{0:T(128)} all-reduce(f32[1]{0:T(128)} %bitcast.15), channel_id=1, replica_groups=mesh['freq'=2,'base'=4,'pix'=4] {'freq'}, use_global_device_ids=true, to_apply=%region_19.0 | all-reduce | flops 1 | bytes 8 | tf_op jit(solution)/shard_map/psum | solution.py:51
  350.8 19.6 %reduce-scatter.33.cloned.1.call-done = f32[32,256]{1,0:T(8,128)} async-done(((f32[32,1024]{1,0:T(8,128)}), f32[32,256]{1,0:T(8,128)}) %reduce-scatter.33.cloned.1.call-update) | async-done | bytes 32784 | tf_op jit(solution)/shard_map/reduce_scatter | solution.py:23
  371.1 13.1 %all_gather.47 = bf16[32,1024]{1,0:T(8,128)(2,1)S(1)} all-gather(bf16[32,256]{1,0:T(8,128)(2,1)S(1)} %subtract_convert_fusion), channel_id=1, replica_groups=mesh['freq'=2,'base'=4,'pix'=4] {'pix'}, dimensions={1}, use_global_device_ids=true | all-gather | bytes 81920 | tf_op jit(solution)/shard_map/all_gather | solution.py:28
  385.7 17.4 %reduce-scatter.35.cloned.1.call-done = f32[32,128]{1,0:T(8,128)} async-done(((f32[32,512]{1,0:T(8,128)}), f32[32,128]{1,0:T(8,128)}) %reduce-scatter.35.cloned.1.call-update) | async-done | bytes 16400 | tf_op jit(solution)/shard_map/reduce_scatter | solution.py:47
  404.5 5.5 %psum.47 = f32[1]{0:T(128)} all-reduce(f32[1]{0:T(128)} %bitcast.18), channel_id=1, replica_groups=mesh['freq'=2,'base'=4,'pix'=4] {'freq'}, use_global_device_ids=true, to_apply=%region_23.0 | all-reduce | flops 1 | bytes 8 | tf_op jit(solution)/shard_map/psum | solution.py:51
  (80 shorter events, 62.2 us)
Async XLA Ops:
  6.5 7.0 %copy-start = (bf16[1,1024,512]{2,1,0:T(8,128)(2,1)S(1)}, bf16[1,1024,512]{2,1,0:T(8,128)(2,1)}, u32[]{:S(2)}) copy-start(bf16[1,1024,512]{2,1,0:T(8,128)(2,1)} %param.4) | copy-start | bytes 3145732
  6.5 29.4 %reduce-scatter.13.cloned.1.call-start = ((), (), s32[]{:S(2)}) async-start(), calls=%async_computation.12 | async-start | bytes 163840 | tf_op jit(solution)/shard_map/reduce_scatter | solution.py:23
  14.5 21.4 %copy-start.1 = (f32[32,1024]{1,0:T(8,128)S(1)}, f32[32,1024]{1,0:T(8,128)}, u32[]{:S(2)}) copy-start(f32[32,1024]{1,0:T(8,128)} %param.5) | copy-start | bytes 393220
  14.6 54.1 %reduce-scatter.15.cloned.1.call-start = ((), (), s32[]{:S(2)}) async-start(), calls=%async_computation.13 | async-start | bytes 81920 | tf_op jit(solution)/shard_map/reduce_scatter | solution.py:47
  50.7 0.7 copy-start.4
  50.7 17.9 %copy-start.2 = (f32[32,1,1,128]{3,2,1,0:T(1,128)S(1)}, f32[32,1,1,128]{3,2,1,0:T(1,128)}, u32[]{:S(2)}) copy-start(f32[32,1,1,128]{3,2,1,0:T(1,128)} %param.6) | copy-start | bytes 49156
  50.8 52.0 %reduce-scatter.17.cloned.1.call-start = ((), (), s32[]{:S(2)}) async-start(), calls=%async_computation.14 | async-start | bytes 163840 | tf_op jit(solution)/shard_map/reduce_scatter | solution.py:23
  70.0 6.8 %copy-start.3 = (f32[32,128]{1,0:T(8,128)S(1)}, f32[32,128]{1,0:T(8,128)}, u32[]{:S(2)}) copy-start(f32[32,128]{1,0:T(8,128)} %reduce-scatter.15.cloned.1.call-done) | copy-start | bytes 49156
  83.2 52.3 %reduce-scatter.19.cloned.1.call-start = ((), (), s32[]{:S(2)}) async-start(), calls=%async_computation.15 | async-start | bytes 81920 | tf_op jit(solution)/shard_map/reduce_scatter | solution.py:47
  117.6 52.1 %reduce-scatter.21.cloned.1.call-start = ((), (), s32[]{:S(2)}) async-start(), calls=%async_computation.16 | async-start | bytes 163840 | tf_op jit(solution)/shard_map/reduce_scatter | solution.py:23
  150.1 52.3 %reduce-scatter.23.cloned.1.call-start = ((), (), s32[]{:S(2)}) async-start(), calls=%async_computation.17 | async-start | bytes 81920 | tf_op jit(solution)/shard_map/reduce_scatter | solution.py:47
  184.5 52.1 %reduce-scatter.25.cloned.1.call-start = ((), (), s32[]{:S(2)}) async-start(), calls=%async_computation.18 | async-start | bytes 163840 | tf_op jit(solution)/shard_map/reduce_scatter | solution.py:23
  217.0 52.3 %reduce-scatter.27.cloned.1.call-start = ((), (), s32[]{:S(2)}) async-start(), calls=%async_computation.19 | async-start | bytes 81920 | tf_op jit(solution)/shard_map/reduce_scatter | solution.py:47
  251.4 52.1 %reduce-scatter.29.cloned.1.call-start = ((), (), s32[]{:S(2)}) async-start(), calls=%async_computation.20 | async-start | bytes 163840 | tf_op jit(solution)/shard_map/reduce_scatter | solution.py:23
  283.9 52.3 %reduce-scatter.31.cloned.1.call-start = ((), (), s32[]{:S(2)}) async-start(), calls=%async_computation.21 | async-start | bytes 81920 | tf_op jit(solution)/shard_map/reduce_scatter | solution.py:47
  318.3 52.1 %reduce-scatter.33.cloned.1.call-start = ((), (), s32[]{:S(2)}) async-start(), calls=%async_computation.22 | async-start | bytes 163840 | tf_op jit(solution)/shard_map/reduce_scatter | solution.py:23
  350.7 52.3 %reduce-scatter.35.cloned.1.call-start = ((), (), s32[]{:S(2)}) async-start(), calls=%async_computation.23 | async-start | bytes 81920 | tf_op jit(solution)/shard_map/reduce_scatter | solution.py:47
  404.5 6.8 %copy-start.5 = (f32[32,128]{1,0:T(8,128)S(1)}, f32[32,128]{1,0:T(8,128)}, u32[]{:S(2)}) copy-start(f32[32,128]{1,0:T(8,128)} %reduce-scatter.35.cloned.1.call-done) | copy-start | bytes 49156
Sparse Core Ops, SparseCore 0:
  14.7 21.1 reduce-scatter.12
  50.9 17.7 reduce-scatter.14
  83.3 19.4 reduce-scatter.16
  117.7 17.7 reduce-scatter.18
  150.2 19.4 reduce-scatter.20
  184.6 17.7 reduce-scatter.22
  217.1 19.4 reduce-scatter.24
  251.5 17.7 reduce-scatter.26
  284.0 19.4 reduce-scatter.28
  318.4 17.7 reduce-scatter.30
  350.9 19.4 reduce-scatter.32
  385.3 17.7 reduce-scatter.34
where the time goes:
time: 420 us; the launch traced here: 419 us
  waiting for transfers between devices  223 us (53%)
  blocking collectives  144 us (34%)
  between operations  21.7 us (5%)
  other arithmetic  17.7 us (4%)
  matrix products  11.8 us (3%)
    reduce_scatter x6, waiting for transfers between devices, residual_of(): lax.psum_scatter(partial_value, 'pix', scatter_dimension=1, tiled=True)  119 us
    reduce_scatter x6, waiting for transfers between devices, on_device(): lax.psum_scatter(gradient_portion, 'base', scatter_dimension=1, tiled=True)  103 us
    all_gather x6, blocking collectives, residual_of(): lax.all_gather((own_rows - shares).astype(jnp.bfloat16), 'pix', axis=1, t...  78.7 us
    psum x6, blocking collectives, on_device(): total = lax.psum(local_sum, 'freq')  33.2 us
    all_gather x6, blocking collectives, on_device(): lax.all_gather(rounded_amount, 'base', axis=1, tiled=True)  32 us
    reduce_sum x6, other arithmetic, on_device(): local_sum = jnp.sum(tiles * tiles, axis=(0, 2))  8.45 us
  transfers between devices with their start and end apart: 12, of which 12 were waited for; matrix products, arithmetic and copies ran while one was open for 1% of the time, Pallas kernels for 0%

commit v1 on v0

v1 whole, which is shorter than its diff:
```python
import functools

import jax
import jax.numpy as jnp
from jax import lax
from jax.experimental import pallas as pl
from jax.experimental.pallas import tpu as pltpu
from jax.sharding import PartitionSpec as P

CH = 64
ITERS = 6

descent_stride = 0.6
lam_shrink = 0.3
eps_norm = 1e-06

MESH = pl.DeviceIdType.MESH


def kernel(
    sizes,
    op_ref, meas_ref, sky_ref, rank_ref, out_ref,
    xr_buf, pred_buf, pred_in, resid_buf, resid_in, grad_buf, grad_in,
    z_buf, z_in, sq_buf, sq_in,
    x_send, x_recv, pred_send, pred_recv, resid_send, resid_recv,
    grad_send, grad_recv, sq_send, sq_recv,
):
    n_freq, n_base, n_pix, keep_count = sizes
    f = lax.axis_index("freq")
    b = lax.axis_index("base")
    p = lax.axis_index("pix")
    chans, share = sky_ref.shape
    width = op_ref.shape[0] // n_pix

    def base_at(o):
        return lax.rem(b + o + n_base, n_base)

    def pix_at(o):
        return lax.rem(p + o + n_pix, n_pix)

    def freq_at(o):
        return lax.rem(f + o, n_freq)

    barrier = pltpu.get_barrier_semaphore()
    greeted = 0
    for o in range(1, n_base):
        pl.semaphore_signal(barrier, inc=1, device_id={"base": base_at(o)}, device_id_type=MESH)
        greeted += 1
    for o in range(1, n_pix):
        pl.semaphore_signal(barrier, inc=1, device_id={"pix": pix_at(o)}, device_id_type=MESH)
        greeted += 1
    for fo in range(1, n_freq):
        for o in range(n_base):
            pl.semaphore_signal(
                barrier, inc=1, device_id={"freq": freq_at(fo), "base": base_at(o)}, device_id_type=MESH
            )
            greeted += 1
    pl.semaphore_wait(barrier, greeted)

    def share_copy(source, step, o):
        return pltpu.make_async_remote_copy(
            src_ref=source, dst_ref=z_in.at[step, o - 1],
            send_sem=x_send.at[o - 1], recv_sem=x_recv.at[step, o - 1],
            device_id={"base": base_at(o)}, device_id_type=MESH,
        )

    def sq_copy(step, fo, o):
        at = (fo - 1) * n_base + o
        return pltpu.make_async_remote_copy(
            src_ref=sq_buf, dst_ref=sq_in.at[step, at],
            send_sem=sq_send.at[at], recv_sem=sq_recv.at[step, at],
            device_id={"freq": freq_at(fo), "base": base_at(o)}, device_id_type=MESH,
        )

    def pred_copy(step, o):
        return pltpu.make_async_remote_copy(
            src_ref=pred_buf.at[o - 1], dst_ref=pred_in.at[step, o - 1],
            send_sem=pred_send.at[o - 1], recv_sem=pred_recv.at[step, o - 1],
            device_id={"pix": pix_at(o)}, device_id_type=MESH,
        )

    def resid_copy(step, o):
        return pltpu.make_async_remote_copy(
            src_ref=resid_buf, dst_ref=resid_in.at[step, o - 1],
            send_sem=resid_send.at[o - 1], recv_sem=resid_recv.at[step, o - 1],
            device_id={"pix": pix_at(o)}, device_id_type=MESH,
        )

    def grad_copy(step, o):
        return pltpu.make_async_remote_copy(
            src_ref=grad_buf.at[base_at(o)], dst_ref=grad_in.at[step, o - 1],
            send_sem=grad_send.at[o - 1], recv_sem=grad_recv.at[step, o - 1],
            device_id={"base": base_at(o)}, device_id_type=MESH,
        )

    def rows_of(at):
        return pl.ds(pl.multiple_of(at * width, width), width)

    if width % 128 == 0:
        own_meas = meas_ref[:, rows_of(p)]
    else:
        own_meas = jnp.zeros((chans, width), jnp.float32)
        for j in range(n_pix):
            own_meas = jnp.where(p == j, meas_ref[:, j * width:(j + 1) * width], own_meas)

    def squares(value):
        return jnp.sum((value * value).reshape(chans // 8, 8, share), axis=0)

    def factor_of(step, tile, total):
        rms = jnp.sqrt(jnp.sum(total, axis=(0, 1), keepdims=True) / (CH * share) + eps_norm)
        keeping = (rank_ref[step, tile] < keep_count).astype(jnp.float32)
        return keeping * rms / (rms + lam_shrink)

    order = sorted(range(1, n_pix), key=lambda o: -min(o, n_pix - o))

    def descend(step, current):
        rounded = jnp.concatenate([xr_buf[j] for j in range(n_base)], axis=1)

        def project(at):
            return lax.dot_general(
                rounded, op_ref[rows_of(at), :], (((1,), (1,)), ((), ())),
                preferred_element_type=jnp.float32,
            )

        for o in order:
            pred_buf[o - 1] = project(pix_at(o))
            pred_copy(step, o).start()
        total = project(p)
        for o in range(1, n_pix):
            pred_copy(step, o).wait()
            total = total + pred_in[step, o - 1]
        resid = (own_meas - total).astype(jnp.bfloat16)
        resid_buf[...] = resid
        for o in order:
            resid_copy(step, o).start()
        grad = jnp.dot(resid, op_ref[rows_of(p), :], preferred_element_type=jnp.float32)
        for o in range(1, n_pix):
            resid_copy(step, o).wait()
            grad = grad + jnp.dot(
                resid_in[step, o - 1], op_ref[rows_of(pix_at(-o)), :],
                preferred_element_type=jnp.float32,
            )
        for j in range(n_base):
            grad_buf[j] = grad[:, j * share:(j + 1) * share]
        for o in range(1, n_base):
            grad_copy(step, o).start()
        own = grad_buf[b]
        for o in range(1, n_base):
            grad_copy(step, o).wait()
            own = own + grad_in[step, o - 1]
        return current + descent_stride * own

    for o in range(1, n_base):
        share_copy(sky_ref, 0, o).start()
    first = sky_ref[...]
    xr_buf[b] = first.astype(jnp.bfloat16)
    for o in range(1, n_base):
        share_copy(sky_ref, 0, o).wait()
        xr_buf[base_at(-o)] = z_in[0, o - 1].astype(jnp.bfloat16)

    def iteration(step, current):
        moved = descend(step, current)
        z_buf[...] = moved
        own_sq = squares(moved)
        sq_buf[...] = own_sq
        for fo in range(1, n_freq):
            for o in reversed(range(n_base)):
                sq_copy(step, fo, o).start()
        for o in range(1, n_base):
            share_copy(z_buf, step + 1, o).start()
        result = None
        for o in range(n_base):
            if o:
                share_copy(z_buf, step + 1, o).wait()
                value = z_in[step + 1, o - 1]
                total = squares(value)
            else:
                value, total = moved, own_sq
            for fo in range(1, n_freq):
                sq_copy(step, fo, o).wait()
                total = total + sq_in[step, (fo - 1) * n_base + o]
            tile = base_at(-o)
            scaled = value * factor_of(step, tile, total)
            xr_buf[tile] = scaled.astype(jnp.bfloat16)
            if o == 0:
                result = scaled
        return result

    current = lax.fori_loop(0, ITERS - 1, iteration, first)
    last = ITERS - 1
    moved = descend(last, current)
    total = squares(moved)
    sq_buf[...] = total
    for fo in range(1, n_freq):
        sq_copy(last, fo, 0).start()
    for fo in range(1, n_freq):
        sq_copy(last, fo, 0).wait()
        total = total + sq_in[last, (fo - 1) * n_base]
    out_ref[...] = moved * factor_of(last, b, total)


def on_device(sensing_operator_parts, sampled_correlations, first_sky_estimate, patch_order_record):
    n_freq, n_base, n_pix = (lax.axis_size(a) for a in ("freq", "base", "pix"))
    chans = sampled_correlations.shape[0]
    share = first_sky_estimate.shape[3]
    op = sensing_operator_parts[0]
    rows, block = op.shape
    width = rows // n_pix
    keep_count = n_base * n_pix // 4
    f32, bf16 = jnp.float32, jnp.bfloat16
    dma = pltpu.SemaphoreType.DMA
    n_sq = (n_freq - 1) * n_base
    vmem = pl.BlockSpec(memory_space=pltpu.VMEM)
    result = pl.pallas_call(
        functools.partial(kernel, (n_freq, n_base, n_pix, keep_count)),
        out_shape=jax.ShapeDtypeStruct((chans, share), f32),
        in_specs=[vmem, vmem, vmem, pl.BlockSpec(memory_space=pltpu.SMEM)],
        out_specs=vmem,
        scratch_shapes=[
            pltpu.VMEM((n_base, chans, share), bf16),
            pltpu.VMEM((n_pix - 1, chans, width), f32),
            pltpu.VMEM((ITERS, n_pix - 1, chans, width), f32),
            pltpu.VMEM((chans, width), bf16),
            pltpu.VMEM((ITERS, n_pix - 1, chans, width), bf16),
            pltpu.VMEM((n_base, chans, share), f32),
            pltpu.VMEM((ITERS, n_base - 1, chans, share), f32),
            pltpu.VMEM((chans, share), f32),
            pltpu.VMEM((ITERS, n_base - 1, chans, share), f32),
            pltpu.VMEM((8, share), f32),
            pltpu.VMEM((ITERS, n_sq, 8, share), f32),
            dma((n_base - 1,)), dma((ITERS, n_base - 1)),
            dma((n_pix - 1,)), dma((ITERS, n_pix - 1)),
            dma((n_pix - 1,)), dma((ITERS, n_pix - 1)),
            dma((n_base - 1,)), dma((ITERS, n_base - 1)),
            dma((n_sq,)), dma((ITERS, n_sq)),
        ],
        compiler_params=pltpu.CompilerParams(collective_id=0, has_side_effects=True),
    )(op, sampled_correlations, first_sky_estimate.reshape(chans, share), patch_order_record)
    return result.reshape(chans, 1, 1, share)


def solution(mesh):
    in_specs = (
        P("freq", "base", "pix"),
        P("freq", "base"),
        P("freq", "pix", "base", None),
        P(None, "pix"),
    )
    out_specs = P("freq", "pix", "base", None)
    return jax.shard_map(
        on_device, mesh=mesh, in_specs=in_specs, out_specs=out_specs, check_vma=False
    )
```

time: 420 us -> 106 us (0.25)
  waiting for transfers between devices: 223 us -> 0 us
  blocking collectives: 144 us -> 0 us
  Pallas kernels: 0 us -> 103 us
  between operations: 21.7 us -> 0.01 us
  other arithmetic: 17.7 us -> 0 us
  matrix products: 11.8 us -> 0 us
    reduce_scatter x12 -> x0, waiting for transfers between devices: 222 us -> none  [the longest x6 119 us: residual_of(): lax.psum_scatter(partial_value, 'pix', scatter_dimension=1, tiled=True)]
    all_gather x12 -> x0, blocking collectives: 111 us -> none  [the longest x6 78.7 us: residual_of(): lax.all_gather((own_rows - shares).astype(jnp.bfloat16), 'pix', axis=1, t...]
    pallas_call x0 -> x1, Pallas kernels: none -> 103 us  [on_device(): pl.pallas_call(functools.partial(kernel, (n_freq, n_base, n_pix, keep_cou...]
    psum x6 -> x0, blocking collectives: 33.2 us -> none  [on_device(): total = lax.psum(local_sum, 'freq')]
    dot_general x12 -> x0, matrix products: 11.8 us -> none  [the longest x6 6.32 us: project_rows(): lax.dot_general(rounded_amount, columns, (((1,), (1,)), ((), ())), prefer...]
    reduce_sum x6 -> x0, other arithmetic: 8.45 us -> none  [on_device(): local_sum = jnp.sum(tiles * tiles, axis=(0, 2))]
    convert_element_type x12 -> x0, other arithmetic: 5.42 us -> none  [the longest x6 4.59 us: residual_of(): (own_rows - shares).astype(jnp.bfloat16)]
  transfers between devices with their start and end apart: 12 -> 0, of which waited for: 12 -> 0; matrix products, arithmetic and copies ran while one was open for 1% -> 0% of each run, Pallas kernels for 0% -> 0%
where the time goes in v1:
time: 106 us; the launch traced here: 105 us
  Pallas kernels  103 us (97%)
  local copies, waits for them, and re-layouts  2.68 us (3%)
    pallas_call x1, Pallas kernels, on_device(): pl.pallas_call(functools.partial(kernel, (n_freq, n_base, n_pix, keep_cou...  103 us
    unnamed x4, local copies, waits for them, and re-layouts  2.68 us

profile of v1, /device:TPU:0, one launch (start us, length us, event | category | flops | bytes accessed | tf_op | source)
XLA Modules:
  0.0 105.5 jit_solution(3363198979543556573)
XLA Ops:
  0.0 0.0 copy-start
  0.0 0.7 copy-done
  0.7 0.7 copy.5.rank_ref
  1.4 102.8 %shard_map.46 = f32[32,128]{1,0:T(8,128)} custom-call(bf16[1024,512]{1,0:T(8,128)(2,1)} %bitcast.5, f32[32,1024]{1,0:T(8,128)} %meas_ref.1, f32[32,128]{1,0:T(8,128)} %bitcast.7, s32[6,4]{1,0:T(8,128)} %copy.5.rank_ref), custom_call_target="tpu_custom_call" | custom-call | tf_op jit(solution)/shard_map/pallas_call | solution.py:214
  104.2 1.3 %copy.8 = f32[32,1,1,128]{3,2,1,0:T(1,128)} copy(f32[32,1,1,128]{3,2,1,0:T(1,128)} %bitcast.6) | data formatting | bytes 32768
Async XLA Ops:
  0.0 0.7 copy-start

commit v2 on v1

--- a/solution.py
+++ b/solution.py
@@ -9,6 +9,7 @@
 
 CH = 64
 ITERS = 6
+PIECES = 2
 
 descent_stride = 0.6
 lam_shrink = 0.3
@@ -19,10 +20,10 @@
 
 def kernel(
     sizes,
-    op_ref, meas_ref, sky_ref, rank_ref, out_ref,
-    xr_buf, pred_buf, pred_in, resid_buf, resid_in, grad_buf, grad_in,
+    op_hbm, meas_ref, sky_ref, rank_ref, out_ref,
+    op_ref, xr_buf, pred_buf, pred_in, grad_buf, grad_in,
     z_buf, z_in, sq_buf, sq_in,
-    x_send, x_recv, pred_send, pred_recv, resid_send, resid_recv,
+    op_sem, x_send, x_recv, pred_send, pred_recv,
     grad_send, grad_recv, sq_send, sq_recv,
 ):
     n_freq, n_base, n_pix, keep_count = sizes
@@ -30,7 +31,7 @@
     b = lax.axis_index("base")
     p = lax.axis_index("pix")
     chans, share = sky_ref.shape
-    width = op_ref.shape[0] // n_pix
+    width = op_ref.shape[0] // PIECES
 
     def base_at(o):
         return lax.rem(b + o + n_base, n_base)
@@ -40,6 +41,9 @@
 
     def freq_at(o):
         return lax.rem(f + o, n_freq)
+
+    load = pltpu.make_async_copy(op_hbm, op_ref, op_sem)
+    load.start()
 
     barrier = pltpu.get_barrier_semaphore()
     greeted = 0
@@ -72,17 +76,11 @@
             device_id={"freq": freq_at(fo), "base": base_at(o)}, device_id_type=MESH,
         )
 
-    def pred_copy(step, o):
-        return pltpu.make_async_remote_copy(
-            src_ref=pred_buf.at[o - 1], dst_ref=pred_in.at[step, o - 1],
-            send_sem=pred_send.at[o - 1], recv_sem=pred_recv.at[step, o - 1],
-            device_id={"pix": pix_at(o)}, device_id_type=MESH,
-        )
-
-    def resid_copy(step, o):
-        return pltpu.make_async_remote_copy(
-            src_ref=resid_buf, dst_ref=resid_in.at[step, o - 1],
-            send_sem=resid_send.at[o - 1], recv_sem=resid_recv.at[step, o - 1],
+    def pred_copy(step, h, o):
+        at = h * (n_pix - 1) + o - 1
+        return pltpu.make_async_remote_copy(
+            src_ref=pred_buf.at[h], dst_ref=pred_in.at[step, at],
+            send_sem=pred_send.at[at], recv_sem=pred_recv.at[step, at],
             device_id={"pix": pix_at(o)}, device_id_type=MESH,
         )
 
@@ -93,22 +91,12 @@
             device_id={"base": base_at(o)}, device_id_type=MESH,
         )
 
-    def rows_of(at):
-        return pl.ds(pl.multiple_of(at * width, width), width)
-
-    if width % 128 == 0:
-        own_meas = meas_ref[:, rows_of(p)]
-    else:
-        own_meas = jnp.zeros((chans, width), jnp.float32)
-        for j in range(n_pix):
-            own_meas = jnp.where(p == j, meas_ref[:, j * width:(j + 1) * width], own_meas)
-
     def squares(value):
         return jnp.sum((value * value).reshape(chans // 8, 8, share), axis=0)
 
     def factor_of(step, tile, total):
         rms = jnp.sqrt(jnp.sum(total, axis=(0, 1), keepdims=True) / (CH * share) + eps_norm)
-        keeping = (rank_ref[step, tile] < keep_count).astype(jnp.float32)
+        keeping = (rank_ref[tile, step] < keep_count).astype(jnp.float32)
         return keeping * rms / (rms + lam_shrink)
 
     order = sorted(range(1, n_pix), key=lambda o: -min(o, n_pix - o))
@@ -116,30 +104,27 @@
     def descend(step, current):
         rounded = jnp.concatenate([xr_buf[j] for j in range(n_base)], axis=1)
 
-        def project(at):
-            return lax.dot_general(
-                rounded, op_ref[rows_of(at), :], (((1,), (1,)), ((), ())),
+        pieces = []
+        for h in range(PIECES):
+            part = lax.dot_general(
+                rounded, op_ref[h * width:(h + 1) * width, :], (((1,), (1,)), ((), ())),
                 preferred_element_type=jnp.float32,
             )
-
-        for o in order:
-            pred_buf[o - 1] = project(pix_at(o))
-            pred_copy(step, o).start()
-        total = project(p)
-        for o in range(1, n_pix):
-            pred_copy(step, o).wait()
-            total = total + pred_in[step, o - 1]
-        resid = (own_meas - total).astype(jnp.bfloat16)
-        resid_buf[...] = resid
-        for o in order:
-            resid_copy(step, o).start()
-        grad = jnp.dot(resid, op_ref[rows_of(p), :], preferred_element_type=jnp.float32)
-        for o in range(1, n_pix):
-            resid_copy(step, o).wait()
-            grad = grad + jnp.dot(
-                resid_in[step, o - 1], op_ref[rows_of(pix_at(-o)), :],
+            pred_buf[h] = part.astype(jnp.bfloat16)
+            for o in order:
+                pred_copy(step, h, o).start()
+            pieces.append(part)
+        grad = None
+        for h in range(PIECES):
+            total = meas_ref[:, h * width:(h + 1) * width] - pieces[h]
+            for o in order[::-1]:
+                pred_copy(step, h, o).wait()
+                total = total - pred_in[step, h * (n_pix - 1) + o - 1].astype(jnp.float32)
+            term = jnp.dot(
+                total.astype(jnp.bfloat16), op_ref[h * width:(h + 1) * width, :],
                 preferred_element_type=jnp.float32,
             )
+            grad = term if grad is None else grad + term
         for j in range(n_base):
             grad_buf[j] = grad[:, j * share:(j + 1) * share]
         for o in range(1, n_base):
@@ -157,6 +142,7 @@
     for o in range(1, n_base):
         share_copy(sky_ref, 0, o).wait()
         xr_buf[base_at(-o)] = z_in[0, o - 1].astype(jnp.bfloat16)
+    load.wait()
 
     def iteration(step, current):
         moved = descend(step, current)
@@ -205,7 +191,8 @@
     share = first_sky_estimate.shape[3]
     op = sensing_operator_parts[0]
     rows, block = op.shape
-    width = rows // n_pix
+    width = rows // PIECES
+    n_pred = PIECES * (n_pix - 1)
     keep_count = n_base * n_pix // 4
     f32, bf16 = jnp.float32, jnp.bfloat16
     dma = pltpu.SemaphoreType.DMA
@@ -214,28 +201,26 @@
     result = pl.pallas_call(
         functools.partial(kernel, (n_freq, n_base, n_pix, keep_count)),
         out_shape=jax.ShapeDtypeStruct((chans, share), f32),
-        in_specs=[vmem, vmem, vmem, pl.BlockSpec(memory_space=pltpu.SMEM)],
+        in_specs=[pl.BlockSpec(memory_space=pl.ANY), vmem, vmem, pl.BlockSpec(memory_space=pltpu.SMEM)],
         out_specs=vmem,
         scratch_shapes=[
+            pltpu.VMEM((rows, block), bf16),
             pltpu.VMEM((n_base, chans, share), bf16),
-            pltpu.VMEM((n_pix - 1, chans, width), f32),
-            pltpu.VMEM((ITERS, n_pix - 1, chans, width), f32),
-            pltpu.VMEM((chans, width), bf16),
-            pltpu.VMEM((ITERS, n_pix - 1, chans, width), bf16),
+            pltpu.VMEM((PIECES, chans, width), bf16),
+            pltpu.VMEM((ITERS, n_pred, chans, width), bf16),
             pltpu.VMEM((n_base, chans, share), f32),
             pltpu.VMEM((ITERS, n_base - 1, chans, share), f32),
             pltpu.VMEM((chans, share), f32),
             pltpu.VMEM((ITERS, n_base - 1, chans, share), f32),
             pltpu.VMEM((8, share), f32),
             pltpu.VMEM((ITERS, n_sq, 8, share), f32),
-            dma((n_base - 1,)), dma((ITERS, n_base - 1)),
-            dma((n_pix - 1,)), dma((ITERS, n_pix - 1)),
-            dma((n_pix - 1,)), dma((ITERS, n_pix - 1)),
+            dma, dma((n_base - 1,)), dma((ITERS, n_base - 1)),
+            dma((n_pred,)), dma((ITERS, n_pred)),
             dma((n_base - 1,)), dma((ITERS, n_base - 1)),
             dma((n_sq,)), dma((ITERS, n_sq)),
         ],
         compiler_params=pltpu.CompilerParams(collective_id=0, has_side_effects=True),
-    )(op, sampled_correlations, first_sky_estimate.reshape(chans, share), patch_order_record)
+    )(op, sampled_correlations, first_sky_estimate.reshape(chans, share), patch_order_record.T)
     return result.reshape(chans, 1, 1, share)
 
 

time: 106 us -> 96 us (0.906)
  Pallas kernels: 103 us -> 94.4 us
  local copies, waits for them, and re-layouts: 2.68 us -> 1.32 us
    pallas_call x1, Pallas kernels: 103 us -> 94.4 us  [on_device(): pl.pallas_call(functools.partial(kernel, (n_freq, n_base, n_pix, keep_cou...]
    unnamed x4 -> x1, local copies, waits for them, and re-layouts: 2.68 us -> 1.32 us
where the time goes in v2:
time: 96 us; the launch traced here: 95.7 us
  Pallas kernels  94.4 us (98%)
  local copies, waits for them, and re-layouts  1.32 us (1%)
    pallas_call x1, Pallas kernels, on_device(): pl.pallas_call(functools.partial(kernel, (n_freq, n_base, n_pix, keep_cou...  94.4 us

profile of v2, /device:TPU:0, one launch (start us, length us, event | category | flops | bytes accessed | tf_op | source)
XLA Modules:
  0.0 95.7 jit_solution(16760141395439832647)
XLA Ops:
  0.0 94.4 %shard_map.46 = f32[32,128]{1,0:T(8,128)} custom-call(bf16[1024,512]{1,0:T(8,128)(2,1)} %bitcast.6, f32[32,1024]{1,0:T(8,128)} %meas_ref.1, f32[32,128]{1,0:T(8,128)} %bitcast.8, s32[4,6]{1,0:T(4,128)} %bitcast.9), custom_call_target="tpu_custom_call" | custom-call | tf_op jit(solution)/shard_map/pallas_call | solution.py:201
  94.4 1.3 %copy.7 = f32[32,1,1,128]{3,2,1,0:T(1,128)} copy(f32[32,1,1,128]{3,2,1,0:T(1,128)} %bitcast.7) | data formatting | bytes 32768

commit v3 on v2

--- a/solution.py
+++ b/solution.py
@@ -9,7 +9,6 @@
 
 CH = 64
 ITERS = 6
-PIECES = 2
 
 descent_stride = 0.6
 lam_shrink = 0.3
@@ -20,18 +19,19 @@
 
 def kernel(
     sizes,
-    op_hbm, meas_ref, sky_ref, rank_ref, out_ref,
-    op_ref, xr_buf, pred_buf, pred_in, grad_buf, grad_in,
+    op_hbm, meas_ref, sky_ref, rank_ref, out_ref, factor_ref,
+    op_ref, xr_buf, grad_buf, grad_in,
     z_buf, z_in, sq_buf, sq_in,
-    op_sem, x_send, x_recv, pred_send, pred_recv,
+    op_sem, x_send, x_recv,
     grad_send, grad_recv, sq_send, sq_recv,
+    merge_buf, *piece_scratch,
 ):
-    n_freq, n_base, n_pix, keep_count = sizes
+    n_freq, n_base, n_pix, keep_count, pieces = sizes
+    pred_buf, pred_in, pred_send, pred_recv = (piece_scratch[i::4] for i in range(4))
     f = lax.axis_index("freq")
     b = lax.axis_index("base")
     p = lax.axis_index("pix")
     chans, share = sky_ref.shape
-    width = op_ref.shape[0] // PIECES
 
     def base_at(o):
         return lax.rem(b + o + n_base, n_base)
@@ -77,11 +77,29 @@
         )
 
     def pred_copy(step, h, o):
-        at = h * (n_pix - 1) + o - 1
-        return pltpu.make_async_remote_copy(
-            src_ref=pred_buf.at[h], dst_ref=pred_in.at[step, at],
-            send_sem=pred_send.at[at], recv_sem=pred_recv.at[step, at],
+        return pltpu.make_async_remote_copy(
+            src_ref=pred_buf[h], dst_ref=pred_in[h].at[step, o - 1],
+            send_sem=pred_send[h].at[o - 1], recv_sem=pred_recv[h].at[step, o - 1],
             device_id={"pix": pix_at(o)}, device_id_type=MESH,
+        )
+
+    beside = p + 1 - 2 * lax.rem(p, 2)
+    across = 3 - p
+    inner = jnp.logical_or(p == 1, p == 2)
+
+    def pair_copy(step):
+        return pltpu.make_async_remote_copy(
+            src_ref=pred_buf[0], dst_ref=pred_in[0].at[step, 0],
+            send_sem=pred_send[0].at[0], recv_sem=pred_recv[0].at[step, 0],
+            device_id={"pix": beside}, device_id_type=MESH,
+        )
+
+    def merged_copy(step, k):
+        target = across + 1 - 2 * lax.rem(across, 2) if k else across
+        return pltpu.make_async_remote_copy(
+            src_ref=merge_buf, dst_ref=pred_in[0].at[step, 1],
+            send_sem=pred_send[0].at[1 + k], recv_sem=pred_recv[0].at[step, 1],
+            device_id={"pix": target}, device_id_type=MESH,
         )
 
     def grad_copy(step, o):
@@ -104,24 +122,47 @@
     def descend(step, current):
         rounded = jnp.concatenate([xr_buf[j] for j in range(n_base)], axis=1)
 
-        pieces = []
-        for h in range(PIECES):
+        parts = []
+        for h, (start, width, merged) in enumerate(pieces):
             part = lax.dot_general(
-                rounded, op_ref[h * width:(h + 1) * width, :], (((1,), (1,)), ((), ())),
+                rounded, op_ref[start:start + width, :], (((1,), (1,)), ((), ())),
                 preferred_element_type=jnp.float32,
             )
-            pred_buf[h] = part.astype(jnp.bfloat16)
-            for o in order:
-                pred_copy(step, h, o).start()
-            pieces.append(part)
+            pred_buf[h][...] = part.astype(jnp.bfloat16)
+            if merged:
+                pair_copy(step).start()
+            else:
+                for o in order:
+                    pred_copy(step, h, o).start()
+            parts.append(part)
+        if pieces[0][2]:
+            pair_copy(step).wait()
+            parts[0] = parts[0] + pred_in[0][step, 0].astype(jnp.float32)
+            merge_buf[...] = parts[0].astype(jnp.bfloat16)
+
+            @pl.when(inner)
+            def _():
+                for k in (1, 0):
+                    merged_copy(step, k).start()
+
         grad = None
-        for h in range(PIECES):
-            total = meas_ref[:, h * width:(h + 1) * width] - pieces[h]
-            for o in order[::-1]:
-                pred_copy(step, h, o).wait()
-                total = total - pred_in[step, h * (n_pix - 1) + o - 1].astype(jnp.float32)
+        for h in [*range(1, len(pieces)), 0] if pieces[0][2] else range(len(pieces)):
+            start, width, merged = pieces[h]
+            total = meas_ref[:, start:start + width] - parts[h]
+            if merged:
+                merged_copy(step, 0).wait_recv()
+                total = total - pred_in[h][step, 1].astype(jnp.float32)
+
+                @pl.when(inner)
+                def _():
+                    for k in (0, 1):
+                        merged_copy(step, k).wait_send()
+            else:
+                for o in order[::-1]:
+                    pred_copy(step, h, o).wait()
+                    total = total - pred_in[h][step, o - 1].astype(jnp.float32)
             term = jnp.dot(
-                total.astype(jnp.bfloat16), op_ref[h * width:(h + 1) * width, :],
+                total.astype(jnp.bfloat16), op_ref[start:start + width, :],
                 preferred_element_type=jnp.float32,
             )
             grad = term if grad is None else grad + term
@@ -182,7 +223,8 @@
     for fo in range(1, n_freq):
         sq_copy(last, fo, 0).wait()
         total = total + sq_in[last, (fo - 1) * n_base]
-    out_ref[...] = moved * factor_of(last, b, total)
+    out_ref[...] = moved
+    factor_ref[...] = jnp.broadcast_to(factor_of(last, b, total), factor_ref.shape)
 
 
 def on_device(sensing_operator_parts, sampled_correlations, first_sky_estimate, patch_order_record):
@@ -191,23 +233,31 @@
     share = first_sky_estimate.shape[3]
     op = sensing_operator_parts[0]
     rows, block = op.shape
-    width = rows // PIECES
-    n_pred = PIECES * (n_pix - 1)
-    keep_count = n_base * n_pix // 4
     f32, bf16 = jnp.float32, jnp.bfloat16
     dma = pltpu.SemaphoreType.DMA
+    if n_pix == 4 and rows % 1024 == 0:
+        eighth = rows // 8
+        pieces = ((0, 3 * eighth, True), (3 * eighth, 2 * eighth, False), (5 * eighth, 3 * eighth, False))
+    else:
+        pieces = tuple((h * rows // 2, rows // 2, False) for h in range(2))
+    piece_scratch = []
+    for _, width, _ in pieces:
+        piece_scratch += [
+            pltpu.VMEM((chans, width), bf16),
+            pltpu.VMEM((ITERS, n_pix - 1, chans, width), bf16),
+            dma((n_pix - 1,)), dma((ITERS, n_pix - 1)),
+        ]
+    keep_count = n_base * n_pix // 4
     n_sq = (n_freq - 1) * n_base
     vmem = pl.BlockSpec(memory_space=pltpu.VMEM)
-    result = pl.pallas_call(
-        functools.partial(kernel, (n_freq, n_base, n_pix, keep_count)),
-        out_shape=jax.ShapeDtypeStruct((chans, share), f32),
+    moved, factor = pl.pallas_call(
+        functools.partial(kernel, (n_freq, n_base, n_pix, keep_count, pieces)),
+        out_shape=[jax.ShapeDtypeStruct((chans, share), f32), jax.ShapeDtypeStruct((1, share), f32)],
         in_specs=[pl.BlockSpec(memory_space=pl.ANY), vmem, vmem, pl.BlockSpec(memory_space=pltpu.SMEM)],
-        out_specs=vmem,
+        out_specs=[vmem, vmem],
         scratch_shapes=[
             pltpu.VMEM((rows, block), bf16),
             pltpu.VMEM((n_base, chans, share), bf16),
-            pltpu.VMEM((PIECES, chans, width), bf16),
-            pltpu.VMEM((ITERS, n_pred, chans, width), bf16),
             pltpu.VMEM((n_base, chans, share), f32),
             pltpu.VMEM((ITERS, n_base - 1, chans, share), f32),
             pltpu.VMEM((chans, share), f32),
@@ -215,13 +265,14 @@
             pltpu.VMEM((8, share), f32),
             pltpu.VMEM((ITERS, n_sq, 8, share), f32),
             dma, dma((n_base - 1,)), dma((ITERS, n_base - 1)),
-            dma((n_pred,)), dma((ITERS, n_pred)),
             dma((n_base - 1,)), dma((ITERS, n_base - 1)),
             dma((n_sq,)), dma((ITERS, n_sq)),
+            pltpu.VMEM((chans, pieces[0][1]), bf16),
+            *piece_scratch,
         ],
         compiler_params=pltpu.CompilerParams(collective_id=0, has_side_effects=True),
     )(op, sampled_correlations, first_sky_estimate.reshape(chans, share), patch_order_record.T)
-    return result.reshape(chans, 1, 1, share)
+    return (moved * factor).reshape(chans, 1, 1, share)
 
 
 def solution(mesh):

time: 96 us -> 91.5 us (0.953)
  Pallas kernels: 94.4 us -> 89.3 us
  other arithmetic: 0 us -> 1.32 us
    pallas_call x1, Pallas kernels: 94.4 us -> 89.3 us  [on_device(): pl.pallas_call(functools.partial(kernel, (n_freq, n_base, n_pix, keep_cou...]
    mul x0 -> x1, other arithmetic: none -> 1.32 us  [on_device(): return (moved * factor).reshape(chans, 1, 1, share)]
where the time goes in v3:
time: 91.5 us; the launch traced here: 91.3 us
  Pallas kernels  89.3 us (98%)
  other arithmetic  1.32 us (1%)
    pallas_call x1, Pallas kernels, on_device(): pl.pallas_call(functools.partial(kernel, (n_freq, n_base, n_pix, keep_cou...  89.3 us

profile of v3, /device:TPU:0, one launch (start us, length us, event | category | flops | bytes accessed | tf_op | source)
XLA Modules:
  0.0 91.3 jit_solution(6301962491002131208)
XLA Ops:
  0.0 89.3 %shard_map.46 = (f32[32,128]{1,0:T(8,128)}, f32[1,128]{1,0:T(1,128)}) custom-call(bf16[1024,512]{1,0:T(8,128)(2,1)} %bitcast.7, f32[32,1024]{1,0:T(8,128)} %meas_ref.1, f32[32,128]{1,0:T(8,128)} %bitcast.8, s32[4,6]{1,0:T(4,128)} %bitcast.9), custom_call_target="tpu_custom_call" | custom-call | tf_op jit(solution)/shard_map/pallas_call | solution.py:253
  89.3 0.0 copy-start
  89.3 0.7 copy-done
  89.9 1.3 %broadcast_multiply_fusion = f32[32,128]{1,0:T(8,128)} fusion(f32[32,128]{1,0:T(8,128)} %get-tuple-element.7, f32[128]{0:T(128)S(1)} %bitcast.10), kind=kLoop, calls=%fused_computation | loop fusion | flops 4096 | bytes 33280 | tf_op jit(solution)/shard_map/mul | solution.py:275
Async XLA Ops:
  89.3 0.7 copy-start

commit v4 on v3

--- a/solution.py
+++ b/solution.py
@@ -19,7 +19,7 @@
 
 def kernel(
     sizes,
-    op_hbm, meas_ref, sky_ref, rank_ref, out_ref, factor_ref,
+    op_hbm, meas_ref, sky_ref, rank_ref, out_ref,
     op_ref, xr_buf, grad_buf, grad_in,
     z_buf, z_in, sq_buf, sq_in,
     op_sem, x_send, x_recv,
@@ -136,7 +136,7 @@
                     pred_copy(step, h, o).start()
             parts.append(part)
         if pieces[0][2]:
-            pair_copy(step).wait()
+            pair_copy(step).wait_recv()
             parts[0] = parts[0] + pred_in[0][step, 0].astype(jnp.float32)
             merge_buf[...] = parts[0].astype(jnp.bfloat16)
 
@@ -152,14 +152,9 @@
             if merged:
                 merged_copy(step, 0).wait_recv()
                 total = total - pred_in[h][step, 1].astype(jnp.float32)
-
-                @pl.when(inner)
-                def _():
-                    for k in (0, 1):
-                        merged_copy(step, k).wait_send()
             else:
                 for o in order[::-1]:
-                    pred_copy(step, h, o).wait()
+                    pred_copy(step, h, o).wait_recv()
                     total = total - pred_in[h][step, o - 1].astype(jnp.float32)
             term = jnp.dot(
                 total.astype(jnp.bfloat16), op_ref[start:start + width, :],
@@ -172,9 +167,24 @@
             grad_copy(step, o).start()
         own = grad_buf[b]
         for o in range(1, n_base):
-            grad_copy(step, o).wait()
+            grad_copy(step, o).wait_recv()
             own = own + grad_in[step, o - 1]
         return current + descent_stride * own
+
+    def drain(step):
+        for h, (_, _, merged) in enumerate(pieces):
+            if merged:
+                pair_copy(step).wait_send()
+
+                @pl.when(inner)
+                def _():
+                    for k in (0, 1):
+                        merged_copy(step, k).wait_send()
+            else:
+                for o in order:
+                    pred_copy(step, h, o).wait_send()
+        for o in range(1, n_base):
+            grad_copy(step, o).wait_send()
 
     for o in range(1, n_base):
         share_copy(sky_ref, 0, o).start()
@@ -195,22 +205,28 @@
                 sq_copy(step, fo, o).start()
         for o in range(1, n_base):
             share_copy(z_buf, step + 1, o).start()
+        drain(step)
         result = None
         for o in range(n_base):
             if o:
-                share_copy(z_buf, step + 1, o).wait()
+                share_copy(z_buf, step + 1, o).wait_recv()
                 value = z_in[step + 1, o - 1]
                 total = squares(value)
             else:
                 value, total = moved, own_sq
             for fo in range(1, n_freq):
-                sq_copy(step, fo, o).wait()
+                sq_copy(step, fo, o).wait_recv()
                 total = total + sq_in[step, (fo - 1) * n_base + o]
             tile = base_at(-o)
             scaled = value * factor_of(step, tile, total)
             xr_buf[tile] = scaled.astype(jnp.bfloat16)
             if o == 0:
                 result = scaled
+        for o in range(1, n_base):
+            share_copy(z_buf, step + 1, o).wait_send()
+        for fo in range(1, n_freq):
+            for o in range(n_base):
+                sq_copy(step, fo, o).wait_send()
         return result
 
     current = lax.fori_loop(0, ITERS - 1, iteration, first)
@@ -220,11 +236,11 @@
     sq_buf[...] = total
     for fo in range(1, n_freq):
         sq_copy(last, fo, 0).start()
+    drain(last)
     for fo in range(1, n_freq):
         sq_copy(last, fo, 0).wait()
         total = total + sq_in[last, (fo - 1) * n_base]
-    out_ref[...] = moved
-    factor_ref[...] = jnp.broadcast_to(factor_of(last, b, total), factor_ref.shape)
+    out_ref[...] = moved * factor_of(last, b, total)
 
 
 def on_device(sensing_operator_parts, sampled_correlations, first_sky_estimate, patch_order_record):
@@ -250,11 +266,11 @@
     keep_count = n_base * n_pix // 4
     n_sq = (n_freq - 1) * n_base
     vmem = pl.BlockSpec(memory_space=pltpu.VMEM)
-    moved, factor = pl.pallas_call(
+    result = pl.pallas_call(
         functools.partial(kernel, (n_freq, n_base, n_pix, keep_count, pieces)),
-        out_shape=[jax.ShapeDtypeStruct((chans, share), f32), jax.ShapeDtypeStruct((1, share), f32)],
+        out_shape=jax.ShapeDtypeStruct((chans, share), f32),
         in_specs=[pl.BlockSpec(memory_space=pl.ANY), vmem, vmem, pl.BlockSpec(memory_space=pltpu.SMEM)],
-        out_specs=[vmem, vmem],
+        out_specs=vmem,
         scratch_shapes=[
             pltpu.VMEM((rows, block), bf16),
             pltpu.VMEM((n_base, chans, share), bf16),
@@ -272,7 +288,7 @@
         ],
         compiler_params=pltpu.CompilerParams(collective_id=0, has_side_effects=True),
     )(op, sampled_correlations, first_sky_estimate.reshape(chans, share), patch_order_record.T)
-    return (moved * factor).reshape(chans, 1, 1, share)
+    return result.reshape(chans, 1, 1, share)
 
 
 def solution(mesh):

time: 91.5 us -> 90.8 us (level)
  other arithmetic: 1.32 us -> 0 us
    mul x1 -> x0, other arithmetic: 1.32 us -> none  [on_device(): return (moved * factor).reshape(chans, 1, 1, share)]
where the time goes in v4:
time: 90.8 us; the launch traced here: 90.6 us
  Pallas kernels  89.3 us (98%)
  local copies, waits for them, and re-layouts  1.32 us (1%)
    pallas_call x1, Pallas kernels, on_device(): pl.pallas_call(functools.partial(kernel, (n_freq, n_base, n_pix, keep_cou...  89.3 us

profile of v4, /device:TPU:0, one launch (start us, length us, event | category | flops | bytes accessed | tf_op | source)
XLA Modules:
  0.0 90.6 jit_solution(10322465633066493315)
XLA Ops:
  0.0 89.3 %shard_map.46 = f32[32,128]{1,0:T(8,128)} custom-call(bf16[1024,512]{1,0:T(8,128)(2,1)} %bitcast.6, f32[32,1024]{1,0:T(8,128)} %meas_ref.1, f32[32,128]{1,0:T(8,128)} %bitcast.8, s32[4,6]{1,0:T(4,128)} %bitcast.9), custom_call_target="tpu_custom_call" | custom-call | tf_op jit(solution)/shard_map/pallas_call | solution.py:269
  89.3 1.3 %copy.7 = f32[32,1,1,128]{3,2,1,0:T(1,128)} copy(f32[32,1,1,128]{3,2,1,0:T(1,128)} %bitcast.7) | data formatting | bytes 32768

commit v5 on v4

--- a/solution.py
+++ b/solution.py
@@ -110,7 +110,7 @@
         )
 
     def squares(value):
-        return jnp.sum((value * value).reshape(chans // 8, 8, share), axis=0)
+        return jnp.sum(value * value, axis=0, keepdims=True)
 
     def factor_of(step, tile, total):
         rms = jnp.sqrt(jnp.sum(total, axis=(0, 1), keepdims=True) / (CH * share) + eps_norm)
@@ -198,13 +198,13 @@
     def iteration(step, current):
         moved = descend(step, current)
         z_buf[...] = moved
+        for o in reversed(range(1, n_base)):
+            share_copy(z_buf, step + 1, o).start()
         own_sq = squares(moved)
         sq_buf[...] = own_sq
         for fo in range(1, n_freq):
             for o in reversed(range(n_base)):
                 sq_copy(step, fo, o).start()
-        for o in range(1, n_base):
-            share_copy(z_buf, step + 1, o).start()
         drain(step)
         result = None
         for o in range(n_base):
@@ -278,8 +278,8 @@
             pltpu.VMEM((ITERS, n_base - 1, chans, share), f32),
             pltpu.VMEM((chans, share), f32),
             pltpu.VMEM((ITERS, n_base - 1, chans, share), f32),
-            pltpu.VMEM((8, share), f32),
-            pltpu.VMEM((ITERS, n_sq, 8, share), f32),
+            pltpu.VMEM((1, share), f32),
+            pltpu.VMEM((ITERS, n_sq, 1, share), f32),
             dma, dma((n_base - 1,)), dma((ITERS, n_base - 1)),
             dma((n_base - 1,)), dma((ITERS, n_base - 1)),
             dma((n_sq,)), dma((ITERS, n_sq)),

time: 90.8 us -> 90 us (level)
  no operation moved by 1% of the time
where the time goes in v5:
time: 90 us; the launch traced here: 89.7 us
  Pallas kernels  88.4 us (98%)
  local copies, waits for them, and re-layouts  1.32 us (1%)
    pallas_call x1, Pallas kernels, on_device(): pl.pallas_call(functools.partial(kernel, (n_freq, n_base, n_pix, keep_cou...  88.4 us

profile of v5, /device:TPU:0, one launch (start us, length us, event | category | flops | bytes accessed | tf_op | source)
XLA Modules:
  0.0 89.7 jit_solution(8357845633007486523)
XLA Ops:
  0.0 88.4 %shard_map.46 = f32[32,128]{1,0:T(8,128)} custom-call(bf16[1024,512]{1,0:T(8,128)(2,1)} %bitcast.6, f32[32,1024]{1,0:T(8,128)} %meas_ref.1, f32[32,128]{1,0:T(8,128)} %bitcast.8, s32[4,6]{1,0:T(4,128)} %bitcast.9), custom_call_target="tpu_custom_call" | custom-call | tf_op jit(solution)/shard_map/pallas_call | solution.py:269
  88.4 1.3 %copy.7 = f32[32,1,1,128]{3,2,1,0:T(1,128)} copy(f32[32,1,1,128]{3,2,1,0:T(1,128)} %bitcast.7) | data formatting | bytes 32768
